TPU v7x, 32 devices: a whole 2x2x4 slice. The times are simulated.
32 devices in a mesh: rep: 4 (over y, x), dom: 8 (over z, core).
Axes of the slice: x: 2, y: 2, z: 4, core: 2. Of those that a mesh axis runs over, the one named last changes fastest.
Arguments:
- node_pos: float32 [3, 16384], P(None, 'dom'), may hold values from -6 to 6
- node_order: int32 [8, 2048], P('dom'), may hold values from 0 to 2047, each once within a row
- facet_centroid: float32 [3, 16384], P(None, 'dom'), may hold values from -6 to 6
- facet_normal: float32 [3, 16384], P(None, 'dom'), may hold values from -6 to 6
- facet_nodes: int32 [3, 16384], P(None, 'dom'), may hold values from 0 to 2047
- pair_bucket: int32 [4, 8, 128], P('rep', 'dom'), may hold values from 0 to 15
- pair_owner: int32 [4, 8, 128, 1], P('rep', 'dom'), may hold values from 0 to 7; in each aligned block of 128 rows (0 to 127, 128 to 255, ..., all dimensions but the last counted through in order) at most 32 rows name the same one
- pair_slot: int32 [4, 8, 128], P('rep', 'dom'), may hold values from 0 to 15
- pair_count: int32 [4, 8], P('rep', 'dom'), may hold values from 64 to 128, as said below
Outputs:
- node_force: float32 [3, 16384], P(None, 'dom')
Inputs may be any that keep to these rules, and one draw needn't show every extreme that they name: `pair_owner`: among the 128 pairs of one device, each domain is named at most 32 times, and exactly 32 times in some device's pairs. `pair_count`: some device uses all 128 pairs. `node_order`: each row is a permutation.
All inputs are finite; a program needn't handle non-finite values.
Results may differ from a plain program's by a relative error of at most 0.00013.
Values sent between devices are 32-bit elements; how exact they have to be, the bound alone decides.
A program may use at most 64 MiB of HBM per device.

v0:
```python
import jax
import jax.numpy as jnp
from jax import lax
from jax.sharding import PartitionSpec as P

BUCKET = 128
PAIRS_DEV = 128
STIFFNESS = 0.125
RADIUS_SQ = 4.0
pair_block = 8


def tile_terms(facet_geom, node_points):
    centre = facet_geom[:, 0:3]
    normal = facet_geom[:, 3:6]
    delta = node_points[:, :, None, :] - centre[:, :, :, None]
    gap = jnp.sum(normal[:, :, :, None] * delta, axis=1)
    dist = jnp.sum(delta * delta, axis=1)
    strength = STIFFNESS * jax.nn.softplus(-gap) * jnp.exp(-dist / RADIUS_SQ)
    node_term = jnp.einsum("bkf,bfp->bkp", normal, strength, precision=lax.Precision.HIGHEST)
    reaction = -normal * jnp.sum(strength, axis=2)[:, None, :]
    return (node_term, reaction)


def slot_numbers(owners, is_live, per_owner, dummy_slot):
    rows = owners.shape[0]
    positions = jnp.arange(rows, dtype=jnp.int32)
    earlier = (
        (positions[None, :] < positions[:, None])
        & (owners[None, :] == owners[:, None])
        & is_live[None, :]
    )
    ranking = jnp.sum(earlier.astype(jnp.int32), axis=1)
    return jnp.where(is_live, owners * per_owner + ranking, dummy_slot)


def pair_loop(
    live_count, geom_rows, point_rows, slot_index, bucket_index, is_live, slot_total, bucket_total
):
    width = geom_rows.shape[2]
    geom_pad = jnp.concatenate([geom_rows, jnp.zeros((pair_block, 6, width), jnp.float32)], 0)
    point_pad = jnp.concatenate([point_rows, jnp.zeros((pair_block, 3, width), jnp.float32)], 0)
    slot_pad = jnp.concatenate([slot_index, jnp.full((pair_block,), slot_total, jnp.int32)])
    bucket_pad = jnp.concatenate([bucket_index, jnp.zeros((pair_block,), jnp.int32)])
    live_pad = jnp.concatenate([is_live, jnp.zeros((pair_block,), jnp.bool_)])

    def step(block_index, carry):
        slot_acc, bucket_acc = carry
        start = block_index * pair_block
        facet_geom = lax.dynamic_slice_in_dim(geom_pad, start, pair_block)
        node_points = lax.dynamic_slice_in_dim(point_pad, start, pair_block)
        slot_take = lax.dynamic_slice_in_dim(slot_pad, start, pair_block)
        bucket_take = lax.dynamic_slice_in_dim(bucket_pad, start, pair_block)
        weight = lax.dynamic_slice_in_dim(live_pad, start, pair_block).astype(jnp.float32)
        node_term, reaction = tile_terms(facet_geom, node_points)
        slot_acc = slot_acc.at[slot_take].add(node_term * weight[:, None, None])
        bucket_acc = bucket_acc.at[bucket_take].add(reaction * weight[:, None, None])
        return (slot_acc, bucket_acc)

    blocks = (live_count + pair_block - 1) // pair_block
    start_acc = (
        jnp.zeros((slot_total + 1, 3, width), jnp.float32),
        jnp.zeros((bucket_total, 3, width), jnp.float32),
    )
    return lax.fori_loop(jnp.int32(0), blocks, step, start_acc)


def per_device(
    node_pos,
    node_order,
    facet_centroid,
    facet_normal,
    facet_nodes,
    pair_bucket,
    pair_owner,
    pair_slot,
    pair_count,
):
    domains = lax.axis_size("dom")
    per_owner = max(2, 2 * PAIRS_DEV // domains)
    slot_total = domains * per_owner
    width = BUCKET
    node_buckets = node_pos.shape[1] // width
    facet_buckets = facet_centroid.shape[1] // width
    bucket_points = node_pos[:, node_order[0]].reshape(3, node_buckets, width).transpose(1, 0, 2)
    bucket_geom = (
        jnp.concatenate([facet_centroid, facet_normal], 0)
        .reshape(6, facet_buckets, width)
        .transpose(1, 0, 2)
    )
    owners = pair_owner[0, 0, :, 0]
    buckets = pair_bucket[0, 0]
    slots = pair_slot[0, 0]
    rows = buckets.shape[0]
    positions = jnp.arange(rows, dtype=jnp.int32)
    is_live = positions < pair_count[0, 0]
    live_count = jnp.sum(is_live.astype(jnp.int32))
    slot_index = slot_numbers(owners, is_live, per_owner, slot_total)
    request = (
        jnp.full((slot_total + 1,), -1, jnp.int32)
        .at[slot_index]
        .set(slots)[:-1]
        .reshape(domains, per_owner)
    )
    every_bucket = lax.all_gather(bucket_points, "dom", axis=0, tiled=True)
    point_rows = every_bucket[owners * node_buckets + slots]
    slot_acc, facet_acc = pair_loop(
        live_count,
        bucket_geom[buckets],
        point_rows,
        slot_index,
        buckets,
        is_live,
        slot_total,
        facet_buckets,
    )
    home_blocks, home_slots = (
        lax.all_to_all(
            slot_acc[:-1].reshape(domains, per_owner, 3, width),
            "dom",
            split_axis=0,
            concat_axis=0,
            tiled=True,
        ),
        lax.all_to_all(request.astype(jnp.float32), "dom", split_axis=0, concat_axis=0, tiled=True),
    )
    home_slots = home_slots.reshape(slot_total).astype(jnp.int32)
    home_blocks = home_blocks.reshape(slot_total, 3, width)
    target = jnp.where(home_slots >= 0, home_slots, node_buckets)
    bucket_force = (
        jnp.zeros((node_buckets + 1, 3, width), jnp.float32).at[target].add(home_blocks)[:-1]
    )
    node_force = (
        jnp.zeros((3, node_pos.shape[1]), jnp.float32)
        .at[:, node_order[0]]
        .add(bucket_force.transpose(1, 0, 2).reshape(3, -1))
    )
    reaction = facet_acc.transpose(1, 0, 2).reshape(3, -1) / 3.0
    for corner in range(3):
        node_force = node_force.at[:, facet_nodes[corner]].add(reaction)
    return lax.psum(node_force, "rep")


def solution(mesh):
    placed = (
        P(None, "dom"),
        P("dom", None),
        P(None, "dom"),
        P(None, "dom"),
        P(None, "dom"),
        P("rep", "dom", None),
        P("rep", "dom", None, None),
        P("rep", "dom", None),
        P("rep", "dom"),
    )
    return jax.shard_map(
        per_device, mesh=mesh, in_specs=placed, out_specs=P(None, "dom"), check_vma=False
    )
```

profile of v0, /device:TPU:0, one launch (start us, length us, event | category | flops | bytes accessed | tf_op | source)
XLA Modules:
  0.0 215.3 jit_solution(11657129899521065713)
XLA Ops:
  0.7 0.9 convert_reduce_fusion
  2.3 1.1 scatter_custom_fusion.2
  4.1 6.4 %all-to-all-start = ((f32[8,1,32]{2,1,0:T(1,128)}), f32[8,1,32]{2,1,0:T(1,128)S(1)}, u32[]{:S(2)}, u32[]{:S(2)}) async-start(f32[8,1,32]{2,1,0:T(1,128)} %convert_element_type.37), calls=%async_computation | async-start | bytes 8192 | tf_op jit(solution)/shard_map/all_to_all | solution.py:125
  12.4 1.1 copy.46
  13.5 5.5 %gather_fusion.1 = f32[2048,3]{1,0:T(8,128)S(1)} fusion(f32[3,2048]{0,1:T(8,128)S(1)} %copy.46, s32[2048]{0:T(1024)S(1)} %broadcast_clamp_fusion), kind=kCustom, calls=%fused_computation.1 | custom fusion | bytes 57344 | tf_op jit(solution)/shard_map/gather | solution.py:85
  19.3 14.8 %all_gather.3 = f32[128,3,128]{2,0,1:T(8,128)S(1)} all-gather(f32[16,3,128]{2,0,1:T(8,128)S(1)} %bitcast.77), channel_id=1, replica_groups=mesh['rep'=4,'dom'=8] {'dom'}, dimensions={0}, use_global_device_ids=true | all-gather | bytes 221184 | tf_op jit(solution)/shard_map/all_gather | solution.py:105
  36.1 62.5 %while.12 = (s32[]{:T(128)}, f32[257,3,128]{2,1,0:T(4,128)S(1)}, f32[16,3,128]{2,1,0:T(4,128)S(1)}, s32[]{:T(128)}, s32[136]{0:T(256)S(1)}, /*index=5*/f32[136,6...) while((s32[]{:T(128)}, f32[257,3,128]{2,1,0:T(4,128)S(1)}, ...), condition=%wide.region_9.10_spmd, body=%wide.region_3.9_spmd.sunk | while | flops 8012863 | bytes 3387895 | solution.py:65
  36.1 1.0 fusion.23
  38.3 0.8 scatter_fusion
  39.2 0.8 scatter_fusion.1
  40.1 1.0 fusion.23
  42.3 0.8 scatter_fusion
  43.1 0.8 scatter_fusion.1
  44.0 1.0 fusion.23
  46.2 0.8 scatter_fusion
  47.0 0.8 scatter_fusion.1
  47.9 1.0 fusion.23
  50.1 0.8 scatter_fusion
  50.9 0.8 scatter_fusion.1
  51.8 1.0 fusion.23
  54.0 0.8 scatter_fusion
  54.8 0.8 scatter_fusion.1
  55.7 1.0 fusion.23
  57.9 0.8 scatter_fusion
  58.7 0.8 scatter_fusion.1
  59.6 1.0 fusion.23
  61.8 0.8 scatter_fusion
  62.6 0.8 scatter_fusion.1
  63.5 1.0 fusion.23
  65.7 0.8 scatter_fusion
  66.5 0.8 scatter_fusion.1
  67.4 1.0 fusion.23
  69.6 0.8 scatter_fusion
  70.5 0.8 scatter_fusion.1
  71.3 1.0 fusion.23
  73.5 0.8 scatter_fusion
  74.4 0.8 scatter_fusion.1
  75.2 1.0 fusion.23
  77.4 0.8 scatter_fusion
  78.3 0.8 scatter_fusion.1
  79.1 1.0 fusion.23
  81.3 0.8 scatter_fusion
  82.2 0.8 scatter_fusion.1
  83.0 1.0 fusion.23
  85.2 0.8 scatter_fusion
  86.1 0.8 scatter_fusion.1
  86.9 1.0 fusion.23
  89.1 0.8 scatter_fusion
  90.0 0.8 scatter_fusion.1
  90.8 1.0 fusion.23
  93.0 0.8 scatter_fusion
  93.9 0.8 scatter_fusion.1
  94.7 1.0 fusion.23
  96.9 0.8 scatter_fusion
  97.8 0.8 scatter_fusion.1
  99.8 3.5 %all-to-all-start.1 = ((f32[8,32,3,128]{3,1,2,0:T(8,128)}), f32[8,32,3,128]{3,1,2,0:T(8,128)S(1)}, u32[]{:S(2)}, u32[]{:S(2)}) async-start(f32[8,32,3,128]{3,1,2,0:T(8,128)} %copy.50), calls=%async_computation.1 | async-start | bytes 786432 | tf_op jit(solution)/shard_map/all_to_all | solution.py:118
  103.5 12.3 %all-to-all-done.1 = f32[8,32,3,128]{3,1,2,0:T(8,128)S(1)} async-done(((f32[8,32,3,128]{3,1,2,0:T(8,128)}), f32[8,32,3,128]{3,1,2,0:T(8,128)S(1)}, u32[]{:S(2)}, u32[]{:S(2)}) %all-to-all-start.1) | async-done | bytes 393248 | tf_op jit(solution)/shard_map/all_to_all | solution.py:118
  116.1 8.9 %scatter_fusion.2 = f32[17,3,128]{2,1,0:T(4,128)S(1)} fusion(f32[17,3,128]{2,1,0:T(4,128)S(1)} %broadcast_in_dim.32, s32[256]{0:T(256)S(1)} %bitcast.84, f32[256,3,128]{2,1,0:T(4,128)S(1)} %copy.52), kind=kCustom, calls=%fused_computation.6 | custom fusion | flops 98304 | bytes 1180672 | tf_op jit(solution)/shard_map/scatter-add | solution.py:131
  125.3 11.7 %scatter_custom_fusion.4 = f32[3,2048]{0,1:T(8,128)S(1)} fusion(s32[2048]{0:T(1024)S(1)} %bitcast.82, f32[2048,3]{1,0:T(8,128)S(1)} %copy.53, f32[]{:T(128)} %constant.33.clone.1), kind=kCustom, calls=%fused_computation.26 | custom fusion | flops 6144 | bytes 24580 | tf_op jit(solution)/shard_map/scatter-add | solution.py:136
  137.1 11.9 %scatter_fusion.3 = f32[3,2048]{0,1:T(8,128)S(1)} fusion(f32[3,2048]{0,1:T(8,128)S(1)} %scatter_custom_fusion.4, s32[2048]{0:T(1024)S(1)} %bitcast.80, f32[2048,3]{1,0:T(8,128)S(1)} %copy.54), kind=kCustom, calls=%fused_computation.8 | custom fusion | flops 6144 | bytes 81920 | tf_op jit(solution)/shard_map/scatter-add | solution.py:140
  148.9 12.1 %scatter_fusion.4 = f32[3,2048]{0,1:T(8,128)S(1)} fusion(f32[3,2048]{0,1:T(8,128)S(1)} %scatter_fusion.3, s32[2048]{0:T(1024)S(1)} %bitcast.79, f32[2048,3]{1,0:T(8,128)S(1)} %copy.54), kind=kCustom, calls=%fused_computation.9 | custom fusion | flops 6144 | bytes 81920 | tf_op jit(solution)/shard_map/scatter-add | solution.py:140
  161.0 11.9 %scatter_fusion.5 = f32[3,2048]{0,1:T(8,128)S(1)} fusion(f32[3,2048]{0,1:T(8,128)S(1)} %scatter_fusion.4, s32[2048]{0:T(1024)S(1)} %bitcast.78, f32[2048,3]{1,0:T(8,128)S(1)} %copy.54), kind=kCustom, calls=%fused_computation.10 | custom fusion | flops 6144 | bytes 81920 | tf_op jit(solution)/shard_map/scatter-add | solution.py:140
  172.9 41.5 %psum.7 = f32[3,2048]{0,1:T(8,128)S(1)} all-reduce(f32[3,2048]{0,1:T(8,128)S(1)} %scatter_fusion.5), channel_id=1, replica_groups=mesh['rep'=4,'dom'=8] {'rep'}, use_global_device_ids=true, to_apply=%region_15.16 | all-reduce | flops 6144 | bytes 49152 | tf_op jit(solution)/shard_map/psum | solution.py:141
  214.4 0.9 copy.57
  (144 shorter events, 26.9 us)
Async XLA Ops:
  4.1 95.8 %all-to-all-start = ((f32[8,1,32]{2,1,0:T(1,128)}), f32[8,1,32]{2,1,0:T(1,128)S(1)}, u32[]{:S(2)}, u32[]{:S(2)}) async-start(f32[8,1,32]{2,1,0:T(1,128)} %convert_element_type.37), calls=%async_computation | async-start | bytes 8192 | tf_op jit(solution)/shard_map/all_to_all | solution.py:125
  13.5 20.7 %copy-start.3 = (s32[1,1,128,1]{2,3,1,0:T(1,128)S(1)}, s32[1,1,128,1]{2,3,1,0:T(1,128)}, u32[]{:S(2)}) copy-start(s32[1,1,128,1]{2,3,1,0:T(1,128)} %param.17) | copy-start | bytes 1540
  13.5 20.8 %copy-start.4 = (s32[1,1,128]{2,1,0:T(1,128)S(1)}, s32[1,1,128]{2,1,0:T(1,128)}, u32[]{:S(2)}) copy-start(s32[1,1,128]{2,1,0:T(1,128)} %param.16) | copy-start | bytes 1540
  19.3 15.8 %copy-start = (f32[3,2048]{1,0:T(4,128)S(1)}, f32[3,2048]{1,0:T(4,128)}, u32[]{:S(2)}) copy-start(f32[3,2048]{1,0:T(4,128)} %param.14) | copy-start | bytes 73732
  19.3 15.8 %copy-start.1 = (f32[3,2048]{1,0:T(4,128)S(1)}, f32[3,2048]{1,0:T(4,128)}, u32[]{:S(2)}) copy-start(f32[3,2048]{1,0:T(4,128)} %param.13) | copy-start | bytes 73732
  99.5 3.9 %copy-start.2 = (s32[3,2048]{1,0:T(4,128)S(1)}, s32[3,2048]{1,0:T(4,128)}, u32[]{:S(2)}) copy-start(s32[3,2048]{1,0:T(4,128)} %param.15) | copy-start | bytes 73732
  99.8 15.9 %all-to-all-start.1 = ((f32[8,32,3,128]{3,1,2,0:T(8,128)}), f32[8,32,3,128]{3,1,2,0:T(8,128)S(1)}, u32[]{:S(2)}, u32[]{:S(2)}) async-start(f32[8,32,3,128]{3,1,2,0:T(8,128)} %copy.50), calls=%async_computation.1 | async-start | bytes 786432 | tf_op jit(solution)/shard_map/all_to_all | solution.py:118
where the time goes:
time: 216 us; the launch traced here: 215 us
  other arithmetic  112 us (52%)
  blocking collectives  56.2 us (26%)
  local copies, waits for them, and re-layouts  13.8 us (6%)
  waiting for transfers between devices  12.3 us (6%)
  starting transfers between devices  9.82 us (5%)
  matrix products  8.35 us (4%)
    psum x1, blocking collectives, per_device(): return lax.psum(node_force, 'rep')  41.5 us
    scatter-add x3, other arithmetic, per_device(): node_force = node_force.at[:, facet_nodes[corner]].add(reaction)  35.8 us
    reduce_sum x16, other arithmetic, tile_terms(): gap = jnp.sum(normal[:, :, :, None] * delta, axis=1)  16.6 us
    all_gather x1, blocking collectives, per_device(): every_bucket = lax.all_gather(bucket_points, 'dom', axis=0, tiled=True)  14.8 us
    scatter-add x16, other arithmetic, step(): slot_acc = slot_acc.at[slot_take].add(node_term * weight[:, None, None])  12.5 us
    scatter-add x16, other arithmetic, step(): bucket_acc.at[bucket_take].add(reaction * weight[:, None, None])  12.5 us
    all_to_all x1, waiting for transfers between devices, per_device(): lax.all_to_all(slot_acc[:-1].reshape(domains, per_owner, 3, width), 'dom'...  12.3 us
    scatter-add x1, other arithmetic, per_device(): node_force = jnp.zeros((3, node_pos.shape[1]), jnp.float32).at[:, node_or...  11.7 us
  transfers between devices with their start and end apart: 2, of which 1 were waited for; matrix products, arithmetic and copies ran while one was open for 34% of the time, Pallas kernels for 0%

commit v1 on v0

--- a/solution.py
+++ b/solution.py
@@ -102,7 +102,15 @@
         .set(slots)[:-1]
         .reshape(domains, per_owner)
     )
-    every_bucket = lax.all_gather(bucket_points, "dom", axis=0, tiled=True)
+    size = lax.axis_size("dom")
+    moving, pieces = (bucket_points, [bucket_points])
+    for _ in range(size - 1):
+        moving = lax.ppermute(moving, "dom", [(i, (i + 1) % size) for i in range(size)])
+        pieces.insert(0, moving)
+    row_of_blocks = jnp.concatenate(pieces, axis=0)
+    every_bucket = jnp.roll(
+        row_of_blocks, (lax.axis_index("dom") + 1) * bucket_points.shape[0], axis=0
+    )
     point_rows = every_bucket[owners * node_buckets + slots]
     slot_acc, facet_acc = pair_loop(
         live_count,

time: 216 us -> 226 us (1.046)
  waiting for transfers between devices: 12.3 us -> 38.9 us
  blocking collectives: 56.2 us -> 41.3 us
    ppermute x0 -> x7, waiting for transfers between devices: none -> 26.9 us  [per_device(): lax.ppermute(moving, 'dom', [(i, (i + 1) % size) for i in range(size)])]
    all_gather x1 -> x0, blocking collectives: 14.8 us -> none  [per_device(): every_bucket = lax.all_gather(bucket_points, 'dom', axis=0, tiled=True)]
  transfers between devices with their start and end apart: 2 -> 9, of which waited for: 1 -> 7; matrix products, arithmetic and copies ran while one was open for 34% -> 30% of each run, Pallas kernels for 0% -> 0%
where the time goes in v1:
time: 226 us; the launch traced here: 225 us
  other arithmetic  111 us (49%)
  blocking collectives  41.3 us (18%)
  waiting for transfers between devices  38.9 us (17%)
  local copies, waits for them, and re-layouts  13.8 us (6%)
  starting transfers between devices  9.3 us (4%)
  matrix products  8.35 us (4%)
    psum x1, blocking collectives, per_device(): return lax.psum(node_force, 'rep')  41.3 us
    scatter-add x3, other arithmetic, per_device(): node_force = node_force.at[:, facet_nodes[corner]].add(reaction)  35.8 us
    ppermute x7, waiting for transfers between devices, per_device(): lax.ppermute(moving, 'dom', [(i, (i + 1) % size) for i in range(size)])  26.9 us
    reduce_sum x16, other arithmetic, tile_terms(): gap = jnp.sum(normal[:, :, :, None] * delta, axis=1)  16.6 us
    scatter-add x16, other arithmetic, step(): slot_acc = slot_acc.at[slot_take].add(node_term * weight[:, None, None])  12.5 us
    scatter-add x16, other arithmetic, step(): bucket_acc.at[bucket_take].add(reaction * weight[:, None, None])  12.5 us
    all_to_all x1, waiting for transfers between devices, per_device(): lax.all_to_all(slot_acc[:-1].reshape(domains, per_owner, 3, width), 'dom'...  12 us
    scatter-add x1, other arithmetic, per_device(): node_force = jnp.zeros((3, node_pos.shape[1]), jnp.float32).at[:, node_or...  11.7 us
  transfers between devices with their start and end apart: 9, of which 7 were waited for; matrix products, arithmetic and copies ran while one was open for 30% of the time, Pallas kernels for 0%

profile of v1, /device:TPU:0, one launch (start us, length us, event | category | flops | bytes accessed | tf_op | source)
XLA Modules:
  0.0 225.1 jit_solution(9492872087476215533)
XLA Ops:
  0.8 1.1 copy.44
  1.9 5.5 %gather_fusion.1 = f32[2048,3]{1,0:T(8,128)S(1)} fusion(f32[3,2048]{0,1:T(8,128)S(1)} %copy.44, s32[2048]{0:T(1024)S(1)} %broadcast_clamp_fusion), kind=kCustom, calls=%fused_computation.1 | custom fusion | bytes 57344 | tf_op jit(solution)/shard_map/gather | solution.py:85
  9.1 1.0 scatter_custom_fusion.2
  10.1 3.8 %collective-permute-done = f32[16,3,128]{2,1,0:T(4,128)S(1)} collective-permute-done((f32[16,3,128]{2,1,0:T(4,128)S(1)}, f32[16,3,128]{2,1,0:T(4,128)S(1)}, u32[]{:S(2)}, u32[]{:S(2)}) %collective-permute-start) | collective-permute-done | bytes 24608 | tf_op jit(solution)/shard_map/ppermute | solution.py:108
  14.6 4.8 %all-to-all-start = ((f32[8,1,32]{2,1,0:T(1,128)}), f32[8,1,32]{2,1,0:T(1,128)S(1)}, u32[]{:S(2)}, u32[]{:S(2)}) async-start(f32[8,1,32]{2,1,0:T(1,128)} %convert_element_type.37), calls=%async_computation | async-start | bytes 8192 | tf_op jit(solution)/shard_map/all_to_all | solution.py:133
  19.9 4.8 %collective-permute-done.2 = f32[16,3,128]{2,1,0:T(4,128)S(1)} collective-permute-done((f32[16,3,128]{2,1,0:T(4,128)S(1)}, f32[16,3,128]{2,1,0:T(4,128)S(1)}, u32[]{:S(2)}, u32[]{:S(2)}) %collective-permute-start.2) | collective-permute-done | bytes 24608 | tf_op jit(solution)/shard_map/ppermute | solution.py:108
  25.3 4.5 %collective-permute-done.3 = f32[16,3,128]{2,1,0:T(4,128)S(1)} collective-permute-done((f32[16,3,128]{2,1,0:T(4,128)S(1)}, f32[16,3,128]{2,1,0:T(4,128)S(1)}, u32[]{:S(2)}, u32[]{:S(2)}) %collective-permute-start.3) | collective-permute-done | bytes 24608 | tf_op jit(solution)/shard_map/ppermute | solution.py:108
  29.8 5.1 %collective-permute-done.4 = f32[16,3,128]{2,1,0:T(4,128)S(1)} collective-permute-done((f32[16,3,128]{2,1,0:T(4,128)S(1)}, f32[16,3,128]{2,1,0:T(4,128)S(1)}, u32[]{:S(2)}, u32[]{:S(2)}) %collective-permute-start.4) | collective-permute-done | bytes 24608 | tf_op jit(solution)/shard_map/ppermute | solution.py:108
  35.0 5.1 %collective-permute-done.5 = f32[16,3,128]{2,1,0:T(4,128)S(1)} collective-permute-done((f32[16,3,128]{2,1,0:T(4,128)S(1)}, f32[16,3,128]{2,1,0:T(4,128)S(1)}, u32[]{:S(2)}, u32[]{:S(2)}) %collective-permute-start.5) | collective-permute-done | bytes 24608 | tf_op jit(solution)/shard_map/ppermute | solution.py:108
  41.6 3.7 %collective-permute-done.6 = f32[16,3,128]{2,1,0:T(4,128)S(1)} collective-permute-done((f32[16,3,128]{2,1,0:T(4,128)S(1)}, f32[16,3,128]{2,1,0:T(4,128)S(1)}, u32[]{:S(2)}, u32[]{:S(2)}) %collective-permute-start.6) | collective-permute-done | bytes 24608 | tf_op jit(solution)/shard_map/ppermute | solution.py:108
  46.5 62.5 %while.12 = (s32[]{:T(128)}, f32[257,3,128]{2,1,0:T(4,128)S(1)}, f32[16,3,128]{2,1,0:T(4,128)S(1)}, s32[]{:T(128)}, s32[136]{0:T(256)S(1)}, /*index=5*/f32[136,6...) while((s32[]{:T(128)}, f32[257,3,128]{2,1,0:T(4,128)S(1)}, ...), condition=%wide.region_9.10_spmd, body=%wide.region_3.9_spmd.sunk | while | flops 8012863 | bytes 3387895 | solution.py:65
  46.6 1.0 fusion.23
  48.8 0.8 scatter_fusion
  49.6 0.8 scatter_fusion.1
  50.5 1.0 fusion.23
  52.7 0.8 scatter_fusion
  53.5 0.8 scatter_fusion.1
  54.4 1.0 fusion.23
  56.6 0.8 scatter_fusion
  57.4 0.8 scatter_fusion.1
  58.3 1.0 fusion.23
  60.5 0.8 scatter_fusion
  61.3 0.8 scatter_fusion.1
  62.2 1.0 fusion.23
  64.4 0.8 scatter_fusion
  66.1 1.0 fusion.23
  68.3 0.8 scatter_fusion
  70.0 1.0 fusion.23
  72.2 0.8 scatter_fusion
  73.0 0.8 scatter_fusion.1
  73.9 1.0 fusion.23
  76.1 0.8 scatter_fusion
  77.8 1.0 fusion.23
  80.0 0.8 scatter_fusion
  80.8 0.8 scatter_fusion.1
  81.7 1.0 fusion.23
  83.9 0.8 scatter_fusion
  84.8 0.8 scatter_fusion.1
  85.6 1.0 fusion.23
  87.8 0.8 scatter_fusion
  88.7 0.8 scatter_fusion.1
  89.5 1.0 fusion.23
  91.7 0.8 scatter_fusion
  92.6 0.8 scatter_fusion.1
  93.4 1.0 fusion.23
  95.6 0.8 scatter_fusion
  96.5 0.8 scatter_fusion.1
  97.3 1.0 fusion.23
  99.5 0.8 scatter_fusion
  100.4 0.8 scatter_fusion.1
  101.2 1.0 fusion.23
  103.4 0.8 scatter_fusion
  105.1 1.0 fusion.23
  107.3 0.8 scatter_fusion
  108.2 0.8 scatter_fusion.1
  109.8 3.5 %all-to-all-start.1 = ((f32[8,32,3,128]{3,1,2,0:T(8,128)}), f32[8,32,3,128]{3,1,2,0:T(8,128)S(1)}, u32[]{:S(2)}, u32[]{:S(2)}) async-start(f32[8,32,3,128]{3,1,2,0:T(8,128)} %copy.47), calls=%async_computation.1 | async-start | bytes 786432 | tf_op jit(solution)/shard_map/all_to_all | solution.py:126
  113.8 12.0 %all-to-all-done.1 = f32[8,32,3,128]{3,1,2,0:T(8,128)S(1)} async-done(((f32[8,32,3,128]{3,1,2,0:T(8,128)}), f32[8,32,3,128]{3,1,2,0:T(8,128)S(1)}, u32[]{:S(2)}, u32[]{:S(2)}) %all-to-all-start.1) | async-done | bytes 393248 | tf_op jit(solution)/shard_map/all_to_all | solution.py:126
  126.1 8.9 %scatter_fusion.2 = f32[17,3,128]{2,1,0:T(4,128)S(1)} fusion(f32[17,3,128]{2,1,0:T(4,128)S(1)} %broadcast_in_dim.32, s32[256]{0:T(256)S(1)} %bitcast.85, f32[256,3,128]{2,1,0:T(4,128)S(1)} %copy.49), kind=kCustom, calls=%fused_computation.6 | custom fusion | flops 98304 | bytes 1180672 | tf_op jit(solution)/shard_map/scatter-add | solution.py:139
  135.3 11.7 %scatter_custom_fusion.4 = f32[3,2048]{0,1:T(8,128)S(1)} fusion(s32[2048]{0:T(1024)S(1)} %bitcast.83, f32[2048,3]{1,0:T(8,128)S(1)} %copy.50, f32[]{:T(128)} %constant.43.clone.1), kind=kCustom, calls=%fused_computation.26 | custom fusion | flops 6144 | bytes 24580 | tf_op jit(solution)/shard_map/scatter-add | solution.py:144
  147.0 11.9 %scatter_fusion.3 = f32[3,2048]{0,1:T(8,128)S(1)} fusion(f32[3,2048]{0,1:T(8,128)S(1)} %scatter_custom_fusion.4, s32[2048]{0:T(1024)S(1)} %bitcast.81, f32[2048,3]{1,0:T(8,128)S(1)} %copy.51), kind=kCustom, calls=%fused_computation.8 | custom fusion | flops 6144 | bytes 81920 | tf_op jit(solution)/shard_map/scatter-add | solution.py:148
  158.9 12.1 %scatter_fusion.4 = f32[3,2048]{0,1:T(8,128)S(1)} fusion(f32[3,2048]{0,1:T(8,128)S(1)} %scatter_fusion.3, s32[2048]{0:T(1024)S(1)} %bitcast.80, f32[2048,3]{1,0:T(8,128)S(1)} %copy.51), kind=kCustom, calls=%fused_computation.9 | custom fusion | flops 6144 | bytes 81920 | tf_op jit(solution)/shard_map/scatter-add | solution.py:148
  171.0 11.9 %scatter_fusion.5 = f32[3,2048]{0,1:T(8,128)S(1)} fusion(f32[3,2048]{0,1:T(8,128)S(1)} %scatter_fusion.4, s32[2048]{0:T(1024)S(1)} %bitcast.79, f32[2048,3]{1,0:T(8,128)S(1)} %copy.51), kind=kCustom, calls=%fused_computation.10 | custom fusion | flops 6144 | bytes 81920 | tf_op jit(solution)/shard_map/scatter-add | solution.py:148
  182.9 41.3 %psum.7 = f32[3,2048]{0,1:T(8,128)S(1)} all-reduce(f32[3,2048]{0,1:T(8,128)S(1)} %scatter_fusion.5), channel_id=1, replica_groups=mesh['rep'=4,'dom'=8] {'rep'}, use_global_device_ids=true, to_apply=%region_15.16 | all-reduce | flops 6144 | bytes 49152 | tf_op jit(solution)/shard_map/psum | solution.py:149
  224.2 0.9 copy.54
  (173 shorter events, 30.6 us)
Async XLA Ops:
  0.7 8.2 %copy-start.3 = (s32[1,1,128,1]{2,3,1,0:T(1,128)S(1)}, s32[1,1,128,1]{2,3,1,0:T(1,128)}, u32[]{:S(2)}) copy-start(s32[1,1,128,1]{2,3,1,0:T(1,128)} %param.17) | copy-start | bytes 1540
  0.7 8.4 %copy-start.4 = (s32[1,1,128]{2,1,0:T(1,128)S(1)}, s32[1,1,128]{2,1,0:T(1,128)}, u32[]{:S(2)}) copy-start(s32[1,1,128]{2,1,0:T(1,128)} %param.18) | copy-start | bytes 1540
  0.7 19.2 %copy-start.2 = (s32[3,2048]{1,0:T(4,128)S(1)}, s32[3,2048]{1,0:T(4,128)}, u32[]{:S(2)}) copy-start(s32[3,2048]{1,0:T(4,128)} %param.15) | copy-start | bytes 73732
  0.8 29.1 %copy-start.5 = (s32[1,1,128]{2,1,0:T(1,128)S(1)}, s32[1,1,128]{2,1,0:T(1,128)}, u32[]{:S(2)}) copy-start(s32[1,1,128]{2,1,0:T(1,128)} %param.16) | copy-start | bytes 1540
  0.8 34.2 %copy-start = (f32[3,2048]{1,0:T(4,128)S(1)}, f32[3,2048]{1,0:T(4,128)}, u32[]{:S(2)}) copy-start(f32[3,2048]{1,0:T(4,128)} %param.14) | copy-start | bytes 73732
  0.8 34.2 %copy-start.1 = (f32[3,2048]{1,0:T(4,128)S(1)}, f32[3,2048]{1,0:T(4,128)}, u32[]{:S(2)}) copy-start(f32[3,2048]{1,0:T(4,128)} %param.13) | copy-start | bytes 73732
  7.7 6.1 %collective-permute-start = (f32[16,3,128]{2,1,0:T(4,128)S(1)}, f32[16,3,128]{2,1,0:T(4,128)S(1)}, u32[]{:S(2)}, u32[]{:S(2)}) collective-permute-start(f32[16,3,128]{2,1,0:T(4,128)S(1)} %bitcast.78), channel_id=1, source_target_pairs={{0,1},{1,2},{2,3},{3,4},{4,5},{5,6},{6,7},{7,0},{8,9},{9,10},{10,1... | collective-permute-start | bytes 73736 | tf_op jit(solution)/shard_map/ppermute | solution.py:108
  13.9 5.5 %collective-permute-start.1 = (f32[16,3,128]{2,1,0:T(4,128)S(1)}, f32[16,3,128]{2,1,0:T(4,128)S(1)}, u32[]{:S(2)}, u32[]{:S(2)}) collective-permute-start(f32[16,3,128]{2,1,0:T(4,128)S(1)} %collective-permute-done), channel_id=1, source_target_pairs={{0,1},{1,2},{2,3},{3,4},{4,5},{5,6},{6,7},{7,0},{8,9},{9,10},{10,1... | collective-permute-start | bytes 73736 | tf_op jit(solution)/shard_map/ppermute | solution.py:108
  14.6 95.3 %all-to-all-start = ((f32[8,1,32]{2,1,0:T(1,128)}), f32[8,1,32]{2,1,0:T(1,128)S(1)}, u32[]{:S(2)}, u32[]{:S(2)}) async-start(f32[8,1,32]{2,1,0:T(1,128)} %convert_element_type.37), calls=%async_computation | async-start | bytes 8192 | tf_op jit(solution)/shard_map/all_to_all | solution.py:133
  19.4 5.3 %collective-permute-start.2 = (f32[16,3,128]{2,1,0:T(4,128)S(1)}, f32[16,3,128]{2,1,0:T(4,128)S(1)}, u32[]{:S(2)}, u32[]{:S(2)}) collective-permute-start(f32[16,3,128]{2,1,0:T(4,128)S(1)} %collective-permute-done.1), channel_id=1, source_target_pairs={{0,1},{1,2},{2,3},{3,4},{4,5},{5,6},{6,7},{7,0},{8,9},{9,10},{10,1... | collective-permute-start | bytes 73736 | tf_op jit(solution)/shard_map/ppermute | solution.py:108
  24.7 5.1 %collective-permute-start.3 = (f32[16,3,128]{2,1,0:T(4,128)S(1)}, f32[16,3,128]{2,1,0:T(4,128)S(1)}, u32[]{:S(2)}, u32[]{:S(2)}) collective-permute-start(f32[16,3,128]{2,1,0:T(4,128)S(1)} %collective-permute-done.2), channel_id=1, source_target_pairs={{0,1},{1,2},{2,3},{3,4},{4,5},{5,6},{6,7},{7,0},{8,9},{9,10},{10,1... | collective-permute-start | bytes 73736 | tf_op jit(solution)/shard_map/ppermute | solution.py:108
  29.8 5.1 %collective-permute-start.4 = (f32[16,3,128]{2,1,0:T(4,128)S(1)}, f32[16,3,128]{2,1,0:T(4,128)S(1)}, u32[]{:S(2)}, u32[]{:S(2)}) collective-permute-start(f32[16,3,128]{2,1,0:T(4,128)S(1)} %collective-permute-done.3), channel_id=1, source_target_pairs={{0,1},{1,2},{2,3},{3,4},{4,5},{5,6},{6,7},{7,0},{8,9},{9,10},{10,1... | collective-permute-start | bytes 73736 | tf_op jit(solution)/shard_map/ppermute | solution.py:108
  35.0 5.1 %collective-permute-start.5 = (f32[16,3,128]{2,1,0:T(4,128)S(1)}, f32[16,3,128]{2,1,0:T(4,128)S(1)}, u32[]{:S(2)}, u32[]{:S(2)}) collective-permute-start(f32[16,3,128]{2,1,0:T(4,128)S(1)} %collective-permute-done.4), channel_id=1, source_target_pairs={{0,1},{1,2},{2,3},{3,4},{4,5},{5,6},{6,7},{7,0},{8,9},{9,10},{10,1... | collective-permute-start | bytes 73736 | tf_op jit(solution)/shard_map/ppermute | solution.py:108
  40.1 5.1 %collective-permute-start.6 = (f32[16,3,128]{2,1,0:T(4,128)S(1)}, f32[16,3,128]{2,1,0:T(4,128)S(1)}, u32[]{:S(2)}, u32[]{:S(2)}) collective-permute-start(f32[16,3,128]{2,1,0:T(4,128)S(1)} %collective-permute-done.5), channel_id=1, source_target_pairs={{0,1},{1,2},{2,3},{3,4},{4,5},{5,6},{6,7},{7,0},{8,9},{9,10},{10,1... | collective-permute-start | bytes 73736 | tf_op jit(solution)/shard_map/ppermute | solution.py:108
  109.8 15.9 %all-to-all-start.1 = ((f32[8,32,3,128]{3,1,2,0:T(8,128)}), f32[8,32,3,128]{3,1,2,0:T(8,128)S(1)}, u32[]{:S(2)}, u32[]{:S(2)}) async-start(f32[8,32,3,128]{3,1,2,0:T(8,128)} %copy.47), calls=%async_computation.1 | async-start | bytes 786432 | tf_op jit(solution)/shard_map/all_to_all | solution.py:126
